TPU v7x, 32 devices: a whole 2x2x4 slice. The times are simulated.
32 devices in a mesh: seq: 8 (over z, x), kvh: 4 (over y, core).
Axes of the slice: x: 2, y: 2, z: 4, core: 2. Of those that a mesh axis runs over, the one named last changes fastest.
Arguments:
- queries: bfloat16 [1024, 28, 128], P('seq', 'kvh'), may hold values from -80 to 80
- new_keys: bfloat16 [1024, 4, 128], P('seq', 'kvh'), may hold values from -8 to 8
- cache_keys: bfloat16 [512, 4, 128], P('seq', 'kvh'), may hold values from -1.1953125 to 1.1953125
- window_start: int32 [8], replicated, may hold values from 0 to 512, as said below
- owner_slot: int32 [8], replicated, may hold values from 0 to 511, as said below
Outputs:
- relevance: bfloat16 [1024, 28, 512], P('seq', 'kvh')
- rep_bank: bfloat16 [512, 4, 128], P('seq', 'kvh')
Inputs may be any that keep to these rules, and one draw needn't show every extreme that they name: `window_start`: each window lies inside the new tokens; some window begins at the first new token and some ends at the last. `owner_slot`: the slots are distinct; the first and the last memory block are always among them.
All inputs are finite; a program needn't handle non-finite values.
Results may differ from a plain program's by a relative error of at most 0.0018.
Values may be sent and summed in bfloat16 or wider, within the bound.
A program may use at most 64 MiB of HBM per device.

v0:
```python
import math
import jax
import jax.numpy as jnp
from jax import lax
from jax.sharding import PartitionSpec as P

BLK = 128
WIN = 512


def row_scores(query_rows, key_rows):
    return lax.dot_general(
        query_rows, key_rows, (((1,), (1,)), ((), ())), preferred_element_type=jnp.float32
    )


def per_device(queries, new_keys, cache_keys, window_start, owner_slot):
    tok_count, group_size, head_dim = queries.shape
    score_scale = 1.0 / math.sqrt(head_dim)
    query_rows = queries.reshape(tok_count * group_size, head_dim)
    device_index = lax.axis_index("seq")
    keys_all = lax.all_gather(new_keys, "seq", axis=0, tiled=True)
    key_flat = keys_all[:, 0, :]
    total_tokens = key_flat.shape[0]
    block_count = total_tokens // BLK
    group_blocks = math.gcd(block_count, 8)
    position = device_index * tok_count + jnp.arange(tok_count, dtype=jnp.int32)
    row_position = jnp.repeat(position, group_size)
    inside = (row_position[:, None] >= window_start[None, :]) & (
        row_position[:, None] < window_start[None, :] + WIN
    )
    inside = inside.astype(jnp.float32)
    key_groups = key_flat.reshape(block_count // group_blocks, group_blocks * BLK, head_dim)
    inside_groups = inside.reshape(
        query_rows.shape[0], block_count // group_blocks, group_blocks
    ).transpose(1, 0, 2)

    def group_sums(members):
        key_part, mask_part = members
        scores = row_scores(query_rows, key_part) * score_scale
        scores = scores.reshape(query_rows.shape[0], group_blocks, BLK)
        softmax_weights = jax.nn.softmax(scores, axis=-1)
        return jnp.einsum("rgk,rg->gk", softmax_weights, mask_part)

    colsum = lax.map(group_sums, (key_groups, inside_groups)).reshape(block_count, BLK)
    colsum = lax.psum(colsum, "seq")
    weights = colsum / (group_size * WIN)
    representative = jnp.einsum(
        "nr,nrz->nz",
        weights,
        key_flat.reshape(block_count, BLK, head_dim).astype(jnp.float32),
        precision=lax.Precision.HIGHEST,
    ).astype(jnp.bfloat16)
    rep_float = representative.astype(jnp.float32)
    local_blocks = cache_keys.shape[0]
    slot_ids = device_index * local_blocks + jnp.arange(local_blocks, dtype=jnp.int32)
    matches = (owner_slot[:, None] == slot_ids[None, :]).astype(jnp.float32)
    placed = jnp.dot(matches.T, rep_float, precision=lax.Precision.HIGHEST)
    slot_taken = jnp.sum(matches, axis=0) > 0.5
    new_shard = jnp.where(slot_taken[:, None], placed.astype(jnp.bfloat16), cache_keys[:, 0, :])
    totals = (
        row_scores(query_rows, lax.all_gather(new_shard, "seq", axis=0, tiled=True)) * score_scale
    )
    relevance = totals.astype(jnp.bfloat16).reshape(tok_count, group_size, totals.shape[1])
    return (relevance, new_shard[:, None, :])


def solution(mesh):
    return jax.shard_map(
        per_device,
        mesh=mesh,
        in_specs=(P("seq", "kvh", None), P("seq", "kvh", None), P("seq", "kvh", None), P(), P()),
        out_specs=(P("seq", "kvh", None), P("seq", "kvh", None)),
        check_vma=False,
    )
```

profile of v0, /device:TPU:0, one launch (start us, length us, event | category | flops | bytes accessed | tf_op | source)
XLA Modules:
  0.0 238.6 jit_solution(1154057495097289812)
XLA Ops:
  0.6 1.1 copy.14
  1.7 0.1 reshape.33
  1.8 32.8 %all_gather.6 = bf16[1024,1,128]{2,0,1:T(8,128)(2,1)S(1)} all-gather(bf16[128,1,128]{2,0,1:T(8,128)(2,1)} %param.6), channel_id=1, replica_groups=mesh['seq'=8,'kvh'=4] {'seq'}, dimensions={0}, use_global_device_ids=true | all-gather | bytes 294912 | tf_op jit(solution)/shard_map/all_gather | solution.py:22
  34.6 0.6 multiply_bitcast_fusion
  35.2 0.9 copy.22
  36.1 145.2 %fusion.12 = (f32[896,8]{1,0:T(8,128)S(1)}, f32[896,8,128]{2,1,0:T(8,128)S(1)}) fusion(f32[896,8,128]{2,1,0:T(8,128)S(1)} %bitcast.27), kind=kOutput, calls=%fused_computation.24 | output fusion | flops 1835135 | bytes 7368704 | tf_op jit(solution)/shard_map/while/body/eval_jaxpr/sub | solution.py:42
  181.3 0.0 copy-start.1
  181.3 0.0 copy-start.3
  181.3 0.0 copy-start.2
  181.4 1.2 broadcast_divide_fusion
  182.6 0.1 broadcast_in_dim.28
  182.7 0.2 ge.15
  182.9 0.0 copy-done.1
  182.9 0.1 and_bitcast_fusion
  183.0 0.5 fusion.1
  183.5 21.4 %psum.7 = f32[8,128]{1,0:T(8,128)S(1)} all-reduce(f32[8,128]{1,0:T(8,128)S(1)} %bitcast.32), channel_id=1, replica_groups=mesh['seq'=8,'kvh'=4] {'seq'}, use_global_device_ids=true, to_apply=%region_3.4 | all-reduce | flops 1024 | bytes 8192 | tf_op jit(solution)/shard_map/psum | solution.py:46
  204.9 0.3 fusion.13
  205.2 0.0 copy-done.3
  205.2 0.1 fusion.8
  205.3 0.0 copy-done.2
  205.3 0.3 fusion.4
  205.6 0.0 copy-start
  205.6 30.5 %all_gather.7 = bf16[512,128]{1,0:T(8,128)(2,1)S(1)} all-gather(bf16[64,128]{1,0:T(8,128)(2,1)S(1)} %fusion.4), channel_id=1, replica_groups=mesh['seq'=8,'kvh'=4] {'seq'}, dimensions={0}, use_global_device_ids=true | all-gather | bytes 147456 | tf_op jit(solution)/shard_map/all_gather | solution.py:62
  236.1 0.4 fusion.3
  236.5 0.5 copy.15
  237.0 0.3 reshape.35
  237.3 1.2 copy.16
  238.6 0.0 copy-done
  (5 shorter events, 0.0 us)
Async XLA Ops:
  181.3 1.6 copy-start.1
  181.3 23.9 %copy-start.3 = (s32[8]{0:T(128)S(1)}, s32[8]{0:T(128)}, u32[]{:S(2)}) copy-start(s32[8]{0:T(128)} %param.9) | copy-start | bytes 100
  181.3 24.0 %copy-start.2 = (bf16[64,1,128]{2,0,1:T(8,128)(2,1)S(1)}, bf16[64,1,128]{2,0,1:T(8,128)(2,1)}, u32[]{:S(2)}) copy-start(bf16[64,1,128]{2,0,1:T(8,128)(2,1)} %param.7) | copy-start | bytes 49156
  205.6 33.0 %copy-start = (bf16[64,128]{1,0:T(8,128)(2,1)}, bf16[64,128]{1,0:T(8,128)(2,1)S(1)}, u32[]{:S(2)}) copy-start(bf16[64,128]{1,0:T(8,128)(2,1)S(1)} %fusion.4) | copy-start | bytes 49156
where the time goes:
time: 239 us
  other arithmetic  147 us (62%)
  blocking collectives  84.7 us (35%)
  local copies, waits for them, and re-layouts  4.46 us (2%)
    sub x1, other arithmetic, group_sums(): softmax_weights = jax.nn.softmax(scores, axis=-1)  145 us
    all_gather x1, blocking collectives, per_device(): keys_all = lax.all_gather(new_keys, 'seq', axis=0, tiled=True)  32.8 us
    all_gather x1, blocking collectives, per_device(): lax.all_gather(new_shard, 'seq', axis=0, tiled=True)  30.5 us
    psum x1, blocking collectives, per_device(): colsum = lax.psum(colsum, 'seq')  21.4 us

commit v1 on v0

--- a/solution.py
+++ b/solution.py
@@ -19,7 +19,12 @@
     score_scale = 1.0 / math.sqrt(head_dim)
     query_rows = queries.reshape(tok_count * group_size, head_dim)
     device_index = lax.axis_index("seq")
-    keys_all = lax.all_gather(new_keys, "seq", axis=0, tiled=True)
+    ring = [new_keys]
+    for hop in range(7):
+        ring.append(lax.ppermute(ring[-1], "seq", [(dev, (dev + 1) % 8) for dev in range(8)]))
+    keys_all = jnp.roll(
+        jnp.concatenate(ring[::-1], axis=0), (lax.axis_index("seq") + 1) * ring[0].shape[0], axis=0
+    )
     key_flat = keys_all[:, 0, :]
     total_tokens = key_flat.shape[0]
     block_count = total_tokens // BLK

time: 239 us -> 104 us (0.44)
  other arithmetic: 147 us -> 2.8 us
  waiting for transfers between devices: 0 us -> 41.5 us
  blocking collectives: 84.7 us -> 47.6 us
  starting transfers between devices: 0 us -> 3.04 us
    sub x1 -> x0, other arithmetic: 145 us -> none  [group_sums(): softmax_weights = jax.nn.softmax(scores, axis=-1)]
    ppermute x0 -> x7, waiting for transfers between devices: none -> 41.5 us  [per_device(): lax.ppermute(ring[-1], 'seq', [(dev, (dev + 1) % 8) for dev in range(8)])]
    all_gather x1 -> x0, blocking collectives: 32.8 us -> none  [per_device(): keys_all = lax.all_gather(new_keys, 'seq', axis=0, tiled=True)]
    psum x1, blocking collectives: 21.4 us -> 17.1 us  [per_device(): colsum = lax.psum(colsum, 'seq')]
    ppermute x0 -> x7, starting transfers between devices: none -> 3.04 us  [per_device(): lax.ppermute(ring[-1], 'seq', [(dev, (dev + 1) % 8) for dev in range(8)])]
  transfers between devices with their start and end apart: 0 -> 7, of which waited for: 0 -> 7; matrix products, arithmetic and copies ran while one was open for 0% -> 3% of each run, Pallas kernels for 0% -> 0%
where the time goes in v1:
time: 104 us
  blocking collectives  47.6 us (46%)
  waiting for transfers between devices  41.5 us (40%)
  local copies, waits for them, and re-layouts  5.48 us (5%)
  starting transfers between devices  3.04 us (3%)
  other arithmetic  2.8 us (3%)
  matrix products  2.45 us (2%)
    ppermute x7, waiting for transfers between devices, per_device(): lax.ppermute(ring[-1], 'seq', [(dev, (dev + 1) % 8) for dev in range(8)])  41.5 us
    all_gather x1, blocking collectives, per_device(): lax.all_gather(new_shard, 'seq', axis=0, tiled=True)  30.5 us
    psum x1, blocking collectives, per_device(): colsum = lax.psum(colsum, 'seq')  17.1 us
    unnamed x23, local copies, waits for them, and re-layouts  3.25 us
    ppermute x7, starting transfers between devices, per_device(): lax.ppermute(ring[-1], 'seq', [(dev, (dev + 1) % 8) for dev in range(8)])  3.04 us
  transfers between devices with their start and end apart: 7, of which 7 were waited for; matrix products, arithmetic and copies ran while one was open for 3% of the time, Pallas kernels for 0%

profile of v1, /device:TPU:0, one launch (start us, length us, event | category | flops | bytes accessed | tf_op | source)
XLA Modules:
  0.0 103.7 jit_solution(3255974162189516865)
XLA Ops:
  0.6 3.0 %collective-permute-start = (bf16[128,1,128]{2,0,1:T(8,128)(2,1)}, bf16[128,1,128]{2,0,1:T(8,128)(2,1)S(1)}, u32[]{:S(2)}, u32[]{:S(2)}) collective-permute-start(bf16[128,1,128]{2,0,1:T(8,128)(2,1)} %param.6), channel_id=1, source_target_pairs={{0,4},{4,8},{8,12},{12,16},{16,20},{20,24},{24,28},{28,0},{1,5},{5... | collective-permute-start | bytes 98312 | tf_op jit(solution)/shard_map/ppermute | solution.py:24
  3.6 5.1 %collective-permute-done = bf16[128,1,128]{2,0,1:T(8,128)(2,1)S(1)} collective-permute-done((bf16[128,1,128]{2,0,1:T(8,128)(2,1)}, bf16[128,1,128]{2,0,1:T(8,128)(2,1)S(1)}, u32[]{:S(2)}, u32[]{:S(2)}) %collective-permute-start) | collective-permute-done | bytes 32800 | tf_op jit(solution)/shard_map/ppermute | solution.py:24
  8.8 0.0 collective-permute-start.1
  8.8 0.7 broadcast_add_fusion
  9.5 6.0 %collective-permute-done.1 = bf16[128,1,128]{2,0,1:T(8,128)(2,1)S(1)} collective-permute-done((bf16[128,1,128]{2,0,1:T(8,128)(2,1)S(1)}, bf16[128,1,128]{2,0,1:T(8,128)(2,1)S(1)}, u32[]{:S(2)}, u32[]{:S(2)}) %collective-permute-start.1) | collective-permute-done | bytes 32800 | tf_op jit(solution)/shard_map/ppermute | solution.py:24
  15.4 0.0 collective-permute-start.2
  15.4 0.1 broadcast_in_dim.28
  15.5 0.2 ge.15
  15.7 6.3 %collective-permute-done.2 = bf16[128,1,128]{2,0,1:T(8,128)(2,1)S(1)} collective-permute-done((bf16[128,1,128]{2,0,1:T(8,128)(2,1)S(1)}, bf16[128,1,128]{2,0,1:T(8,128)(2,1)S(1)}, u32[]{:S(2)}, u32[]{:S(2)}) %collective-permute-start.2) | collective-permute-done | bytes 32800 | tf_op jit(solution)/shard_map/ppermute | solution.py:24
  22.0 0.0 collective-permute-start.3
  22.0 0.7 and_bitcast_fusion
  22.8 5.9 %collective-permute-done.3 = bf16[128,1,128]{2,0,1:T(8,128)(2,1)S(1)} collective-permute-done((bf16[128,1,128]{2,0,1:T(8,128)(2,1)S(1)}, bf16[128,1,128]{2,0,1:T(8,128)(2,1)S(1)}, u32[]{:S(2)}, u32[]{:S(2)}) %collective-permute-start.3) | collective-permute-done | bytes 32800 | tf_op jit(solution)/shard_map/ppermute | solution.py:24
  28.6 0.0 collective-permute-start.4
  28.6 6.9 %collective-permute-done.4 = bf16[128,1,128]{2,0,1:T(8,128)(2,1)S(1)} collective-permute-done((bf16[128,1,128]{2,0,1:T(8,128)(2,1)S(1)}, bf16[128,1,128]{2,0,1:T(8,128)(2,1)S(1)}, u32[]{:S(2)}, u32[]{:S(2)}) %collective-permute-start.4) | collective-permute-done | bytes 32800 | tf_op jit(solution)/shard_map/ppermute | solution.py:24
  35.6 0.0 collective-permute-start.5
  35.6 0.7 fusion.13
  36.3 5.9 %collective-permute-done.5 = bf16[128,1,128]{2,0,1:T(8,128)(2,1)S(1)} collective-permute-done((bf16[128,1,128]{2,0,1:T(8,128)(2,1)S(1)}, bf16[128,1,128]{2,0,1:T(8,128)(2,1)S(1)}, u32[]{:S(2)}, u32[]{:S(2)}) %collective-permute-start.5) | collective-permute-done | bytes 32800 | tf_op jit(solution)/shard_map/ppermute | solution.py:24
  42.2 0.0 collective-permute-start.6
  42.2 1.1 %copy.14 = bf16[128,7,128]{2,1,0:T(8,128)(2,1)S(1)} copy(bf16[128,7,128]{2,0,1:T(8,128)(2,1)} %param.5) | data formatting | bytes 458752 | tf_op args[0]
  43.3 0.1 reshape.33
  43.4 5.4 %collective-permute-done.6 = bf16[128,1,128]{2,0,1:T(8,128)(2,1)S(1)} collective-permute-done((bf16[128,1,128]{2,0,1:T(8,128)(2,1)S(1)}, bf16[128,1,128]{2,0,1:T(8,128)(2,1)S(1)}, u32[]{:S(2)}, u32[]{:S(2)}) %collective-permute-start.6) | collective-permute-done | bytes 32800 | tf_op jit(solution)/shard_map/ppermute | solution.py:24
  48.9 0.8 constant_dynamic-update-slice_fusion.8
  49.8 0.8 constant_dynamic-update-slice_fusion
  50.6 0.6 bitcast_reduce_fusion
  51.2 0.7 fusion.4
  51.9 0.2 broadcast.29
  52.1 0.0 copy-start.1
  52.1 0.0 copy-start.2
  52.1 0.8 fusion.1
  53.0 17.1 %psum.7 = f32[8,128]{1,0:T(8,128)S(1)} all-reduce(f32[8,128]{1,0:T(8,128)S(1)} %bitcast.41), channel_id=1, replica_groups=mesh['seq'=8,'kvh'=4] {'seq'}, use_global_device_ids=true, to_apply=%region_3.4 | all-reduce | flops 1024 | bytes 8192 | tf_op jit(solution)/shard_map/psum | solution.py:51
  70.1 0.3 fusion.17
  70.4 0.0 copy-done.1
  70.4 0.0 copy-done.2
  70.4 0.3 fusion.8
  70.7 0.0 copy-start
  70.7 30.5 %all_gather.3 = bf16[512,128]{1,0:T(8,128)(2,1)S(1)} all-gather(bf16[64,128]{1,0:T(8,128)(2,1)S(1)} %fusion.8), channel_id=1, replica_groups=mesh['seq'=8,'kvh'=4] {'seq'}, dimensions={0}, use_global_device_ids=true | all-gather | bytes 147456 | tf_op jit(solution)/shard_map/all_gather | solution.py:67
  101.2 0.4 fusion.7
  101.6 0.5 copy.15
  102.2 0.3 reshape.35
  102.5 1.2 %copy.16 = bf16[128,7,512]{2,0,1:T(8,128)(2,1)} copy(bf16[128,7,512]{2,1,0:T(8,128)(2,1)S(1)} %reshape.35) | data formatting | bytes 1835008
  103.7 0.0 copy-done
  (19 shorter events, 0.2 us)
Async XLA Ops:
  0.6 8.2 %collective-permute-start = (bf16[128,1,128]{2,0,1:T(8,128)(2,1)}, bf16[128,1,128]{2,0,1:T(8,128)(2,1)S(1)}, u32[]{:S(2)}, u32[]{:S(2)}) collective-permute-start(bf16[128,1,128]{2,0,1:T(8,128)(2,1)} %param.6), channel_id=1, source_target_pairs={{0,4},{4,8},{8,12},{12,16},{16,20},{20,24},{24,28},{28,0},{1,5},{5... | collective-permute-start | bytes 98312 | tf_op jit(solution)/shard_map/ppermute | solution.py:24
  8.8 6.6 %collective-permute-start.1 = (bf16[128,1,128]{2,0,1:T(8,128)(2,1)S(1)}, bf16[128,1,128]{2,0,1:T(8,128)(2,1)S(1)}, u32[]{:S(2)}, u32[]{:S(2)}) collective-permute-start(bf16[128,1,128]{2,0,1:T(8,128)(2,1)S(1)} %collective-permute-done), channel_id=1, source_target_pairs={{0,4},{4,8},{8,12},{12,16},{16,20},{20,24},{24,28},{28,0},{1,5},{5... | collective-permute-start | bytes 98312 | tf_op jit(solution)/shard_map/ppermute | solution.py:24
  15.4 6.6 %collective-permute-start.2 = (bf16[128,1,128]{2,0,1:T(8,128)(2,1)S(1)}, bf16[128,1,128]{2,0,1:T(8,128)(2,1)S(1)}, u32[]{:S(2)}, u32[]{:S(2)}) collective-permute-start(bf16[128,1,128]{2,0,1:T(8,128)(2,1)S(1)} %collective-permute-done.1), channel_id=1, source_target_pairs={{0,4},{4,8},{8,12},{12,16},{16,20},{20,24},{24,28},{28,0},{1,5},{5... | collective-permute-start | bytes 98312 | tf_op jit(solution)/shard_map/ppermute | solution.py:24
  22.0 6.6 %collective-permute-start.3 = (bf16[128,1,128]{2,0,1:T(8,128)(2,1)S(1)}, bf16[128,1,128]{2,0,1:T(8,128)(2,1)S(1)}, u32[]{:S(2)}, u32[]{:S(2)}) collective-permute-start(bf16[128,1,128]{2,0,1:T(8,128)(2,1)S(1)} %collective-permute-done.2), channel_id=1, source_target_pairs={{0,4},{4,8},{8,12},{12,16},{16,20},{20,24},{24,28},{28,0},{1,5},{5... | collective-permute-start | bytes 98312 | tf_op jit(solution)/shard_map/ppermute | solution.py:24
  28.6 7.0 %collective-permute-start.4 = (bf16[128,1,128]{2,0,1:T(8,128)(2,1)S(1)}, bf16[128,1,128]{2,0,1:T(8,128)(2,1)S(1)}, u32[]{:S(2)}, u32[]{:S(2)}) collective-permute-start(bf16[128,1,128]{2,0,1:T(8,128)(2,1)S(1)} %collective-permute-done.3), channel_id=1, source_target_pairs={{0,4},{4,8},{8,12},{12,16},{16,20},{20,24},{24,28},{28,0},{1,5},{5... | collective-permute-start | bytes 98312 | tf_op jit(solution)/shard_map/ppermute | solution.py:24
  35.6 6.6 %collective-permute-start.5 = (bf16[128,1,128]{2,0,1:T(8,128)(2,1)S(1)}, bf16[128,1,128]{2,0,1:T(8,128)(2,1)S(1)}, u32[]{:S(2)}, u32[]{:S(2)}) collective-permute-start(bf16[128,1,128]{2,0,1:T(8,128)(2,1)S(1)} %collective-permute-done.4), channel_id=1, source_target_pairs={{0,4},{4,8},{8,12},{12,16},{16,20},{20,24},{24,28},{28,0},{1,5},{5... | collective-permute-start | bytes 98312 | tf_op jit(solution)/shard_map/ppermute | solution.py:24
  42.2 6.6 %collective-permute-start.6 = (bf16[128,1,128]{2,0,1:T(8,128)(2,1)S(1)}, bf16[128,1,128]{2,0,1:T(8,128)(2,1)S(1)}, u32[]{:S(2)}, u32[]{:S(2)}) collective-permute-start(bf16[128,1,128]{2,0,1:T(8,128)(2,1)S(1)} %collective-permute-done.5), channel_id=1, source_target_pairs={{0,4},{4,8},{8,12},{12,16},{16,20},{20,24},{24,28},{28,0},{1,5},{5... | collective-permute-start | bytes 98312 | tf_op jit(solution)/shard_map/ppermute | solution.py:24
  52.1 18.3 %copy-start.1 = (bf16[64,1,128]{2,0,1:T(8,128)(2,1)S(1)}, bf16[64,1,128]{2,0,1:T(8,128)(2,1)}, u32[]{:S(2)}) copy-start(bf16[64,1,128]{2,0,1:T(8,128)(2,1)} %param.7) | copy-start | bytes 49156
  52.1 18.3 %copy-start.2 = (s32[8]{0:T(128)S(1)}, s32[8]{0:T(128)}, u32[]{:S(2)}) copy-start(s32[8]{0:T(128)} %param.9) | copy-start | bytes 100
  70.7 33.0 %copy-start = (bf16[64,128]{1,0:T(8,128)(2,1)}, bf16[64,128]{1,0:T(8,128)(2,1)S(1)}, u32[]{:S(2)}) copy-start(bf16[64,128]{1,0:T(8,128)(2,1)S(1)} %fusion.8) | copy-start | bytes 49156

commit v2 on v0

--- a/solution.py
+++ b/solution.py
@@ -43,7 +43,7 @@
         return jnp.einsum("rgk,rg->gk", softmax_weights, mask_part)
 
     colsum = lax.map(group_sums, (key_groups, inside_groups)).reshape(block_count, BLK)
-    colsum = lax.psum(colsum, "seq")
+    colsum = jnp.sum(lax.all_gather(colsum, "seq"), axis=0)
     weights = colsum / (group_size * WIN)
     representative = jnp.einsum(
         "nr,nrz->nz",

time: 239 us -> 248 us (1.038)
  blocking collectives: 84.7 us -> 93.9 us
    all_gather x0 -> x1, blocking collectives: none -> 30.6 us  [per_device(): colsum = jnp.sum(lax.all_gather(colsum, 'seq'), axis=0)]
    psum x1 -> x0, blocking collectives: 21.4 us -> none  [per_device(): colsum = lax.psum(colsum, 'seq')]
where the time goes in v2:
time: 248 us
  other arithmetic  147 us (59%)
  blocking collectives  93.9 us (38%)
  local copies, waits for them, and re-layouts  4.46 us (2%)
    sub x1, other arithmetic, group_sums(): softmax_weights = jax.nn.softmax(scores, axis=-1)  145 us
    all_gather x1, blocking collectives, per_device(): keys_all = lax.all_gather(new_keys, 'seq', axis=0, tiled=True)  32.8 us
    all_gather x1, blocking collectives, per_device(): colsum = jnp.sum(lax.all_gather(colsum, 'seq'), axis=0)  30.6 us
    all_gather x1, blocking collectives, per_device(): lax.all_gather(new_shard, 'seq', axis=0, tiled=True)  30.5 us

profile of v2, /device:TPU:0, one launch (start us, length us, event | category | flops | bytes accessed | tf_op | source)
XLA Modules:
  0.0 247.8 jit_solution(2771014542267106605)
XLA Ops:
  0.6 1.1 copy.14
  1.7 0.1 reshape.31
  1.8 32.8 %all_gather.9 = bf16[1024,1,128]{2,0,1:T(8,128)(2,1)S(1)} all-gather(bf16[128,1,128]{2,0,1:T(8,128)(2,1)} %param.6), channel_id=1, replica_groups=mesh['seq'=8,'kvh'=4] {'seq'}, dimensions={0}, use_global_device_ids=true | all-gather | bytes 294912 | tf_op jit(solution)/shard_map/all_gather | solution.py:22
  34.6 0.6 multiply_bitcast_fusion
  35.2 0.9 copy.22
  36.1 145.2 %fusion.12 = (f32[896,8]{1,0:T(8,128)S(1)}, f32[896,8,128]{2,1,0:T(8,128)S(1)}) fusion(f32[896,8,128]{2,1,0:T(8,128)S(1)} %bitcast.29), kind=kOutput, calls=%fused_computation.25 | output fusion | flops 1835135 | bytes 7368704 | tf_op jit(solution)/shard_map/while/body/eval_jaxpr/sub | solution.py:42
  181.3 0.0 copy-start.1
  181.3 0.0 copy-start.3
  181.3 0.0 copy-start.2
  181.4 1.2 broadcast_divide_fusion
  182.6 0.1 broadcast_in_dim.30
  182.7 0.2 ge.15
  182.9 0.0 copy-done.1
  182.9 0.1 and_bitcast_fusion
  183.0 0.5 fusion.1
  183.5 30.6 %all-gather = f32[64,128]{1,0:T(8,128)S(1)} all-gather(f32[8,128]{1,0:T(8,128)S(1)} %bitcast.34), channel_id=2, replica_groups=mesh['seq'=8,'kvh'=4] {'seq'}, dimensions={0}, use_global_device_ids=true | all-gather | bytes 36864 | tf_op jit(solution)/shard_map/all_gather | solution.py:46
  214.1 0.3 fusion.13
  214.4 0.0 copy-done.3
  214.4 0.1 fusion.8
  214.5 0.0 copy-done.2
  214.5 0.3 fusion.4
  214.8 0.0 copy-start
  214.8 30.5 %all_gather.11 = bf16[512,128]{1,0:T(8,128)(2,1)S(1)} all-gather(bf16[64,128]{1,0:T(8,128)(2,1)S(1)} %fusion.4), channel_id=1, replica_groups=mesh['seq'=8,'kvh'=4] {'seq'}, dimensions={0}, use_global_device_ids=true | all-gather | bytes 147456 | tf_op jit(solution)/shard_map/all_gather | solution.py:62
  245.3 0.4 fusion.3
  245.7 0.5 copy.15
  246.3 0.3 reshape.33
  246.6 1.2 copy.16
  247.8 0.0 copy-done
  (6 shorter events, 0.0 us)
Async XLA Ops:
  181.3 1.6 copy-start.1
  181.3 33.1 %copy-start.3 = (s32[8]{0:T(128)S(1)}, s32[8]{0:T(128)}, u32[]{:S(2)}) copy-start(s32[8]{0:T(128)} %param.9) | copy-start | bytes 100
  181.3 33.2 %copy-start.2 = (bf16[64,1,128]{2,0,1:T(8,128)(2,1)S(1)}, bf16[64,1,128]{2,0,1:T(8,128)(2,1)}, u32[]{:S(2)}) copy-start(bf16[64,1,128]{2,0,1:T(8,128)(2,1)} %param.7) | copy-start | bytes 49156
  214.8 33.0 %copy-start = (bf16[64,128]{1,0:T(8,128)(2,1)}, bf16[64,128]{1,0:T(8,128)(2,1)S(1)}, u32[]{:S(2)}) copy-start(bf16[64,128]{1,0:T(8,128)(2,1)S(1)} %fusion.4) | copy-start | bytes 49156
